TPU v7x, 512 devices: a whole 4x8x8 slice. The times are simulated.
512 devices in a mesh: seq: 32 (over x, y), chan: 8 (over z), dp: 2 (over core).
Axes of the slice: x: 4, y: 8, z: 8, core: 2. Of those that a mesh axis runs over, the one named last changes fastest.
Arguments:
- ssm_input: bfloat16 [2, 4096, 4096], P('dp', 'seq', 'chan'), may hold values from -6 to 6
- gate_z: bfloat16 [2, 4096, 4096], P('dp', 'seq', 'chan'), may hold values from -6 to 6
- b_proj: bfloat16 [2, 4096, 128], P('dp', 'seq'), may hold values from -0.52734375 to 0.52734375
- c_proj: bfloat16 [2, 4096, 128], P('dp', 'seq'), may hold values from -6 to 6
- step_size: float32 [2, 4096, 64], P('dp', 'seq', 'chan'), may hold values from 0.02 to 0.2
- log_decay: float32 [2, 4096, 64], P('dp', 'seq', 'chan'), may hold values from -1 to 0, as said below
- skip_d: float32 [64], P('chan'), may hold values from 0.5 to 1.5
- norm_gain: float32 [4096], P('chan'), may hold values from 0.5 to 1.5
- w_out: bfloat16 [4096, 2048], P('chan'), may hold values from -0.09375 to 0.09375
- d_out: bfloat16 [2, 4096, 2048], P('dp', 'seq', 'chan'), may hold values from -6 to 6
- game_lengths: int32 [2, 4], P('dp'), may hold values from 1 to 2048, 4096 in all within a row
Outputs:
- out: bfloat16 [2, 4096, 2048], P('dp', 'seq', 'chan')
- grad_x: bfloat16 [2, 4096, 4096], P('dp', 'seq', 'chan')
- grad_gain: float32 [4096], P('chan')
- grad_skip: float32 [64], P('chan')
Inputs may be any that keep to these rules, and one draw needn't show every extreme that they name: `game_lengths`: each row's 4 game lengths sum to 4096, and the longest is exactly 2048. `log_decay`: a log decay per position and head.
All inputs are finite; a program needn't handle non-finite values.
Results may differ from a plain program's by a relative error of at most 0.017.
Values may be sent and summed in bfloat16 or wider, within the bound.
A program may use at most 64 MiB of HBM per device.

v0:
```python
import jax
import jax.numpy as jnp
from jax import lax
from jax.sharding import Mesh
from jax.sharding import PartitionSpec as P

SEQ = ("seq_0", "seq_1")
SEQ_DP = ("seq_0", "seq_1", "dp")
NORM_EPS = 1e-05


def filled_with(value, identity):
    return jax.tree.map(
        lambda part, zero: jnp.zeros_like(part) + jnp.asarray(zero, part.dtype), value, identity
    )


def prefix_by_axis(value, axes, combine, identity, reverse):
    before = start = filled_with(value, identity)
    so_far = value
    for axis in reversed(axes):
        length, mine = (lax.axis_size(axis), lax.axis_index(axis))
        pieces = jax.tree.map(
            lambda part, kind: lax.all_gather(part.astype(kind), axis),
            so_far,
            (jnp.bfloat16, jnp.bfloat16),
        )
        inside, so_far = (start, start)
        for k in reversed(range(length)) if reverse else range(length):
            passed = k > mine if reverse else k < mine
            so_far = combine(
                so_far, jax.tree.map(lambda part, own: part[k].astype(own.dtype), pieces, value)
            )
            inside = jax.tree.map(lambda new, old: jnp.where(passed, new, old), so_far, inside)
        before = combine(inside, before)
    return before


def in_blocks(value, dim, length):
    lengths = value.shape
    pieces = value.reshape(*lengths[:dim], length, lengths[dim] // length, *lengths[dim + 1 :])
    return jnp.moveaxis(pieces, dim, 0)


def sent_and_summed(value, axis, dim):
    length = lax.axis_size(axis)
    pieces = lax.all_to_all(in_blocks(value, dim, length), axis, 0, 0, tiled=True)
    return jnp.sum(pieces.astype(jnp.float32), axis=0)


def copy_for_each(value, axis):
    length = lax.axis_size(axis)
    return lax.all_to_all(
        jnp.broadcast_to(value[None], (length, *value.shape)), axis, 0, 0, tiled=True
    )


def taken_together(value, axis):
    return copy_for_each(value, axis).sum(axis=0)


def block_parts(c_block, b_block, dt_block, decay_block, reset_block):
    block_len = c_block.shape[0]
    running = jnp.cumsum(decay_block, axis=0)
    reset_count = jnp.cumsum(reset_block, axis=0)
    scores = lax.dot_general(
        c_block, b_block, (((1,), (1,)), ((), ())), preferred_element_type=jnp.float32
    )
    indices = jnp.arange(block_len, dtype=jnp.int32)
    allowed = (indices[:, None] >= indices[None, :]) & (
        reset_count[:, None] == reset_count[None, :]
    )
    log_gap = running.T[:, :, None] - running.T[:, None, :]
    mixing = (
        jnp.where(allowed[None], jnp.exp(jnp.minimum(log_gap, 0.0)), 0.0)
        * scores[None]
        * dt_block.T[:, None, :]
    )
    mixing = mixing.astype(jnp.bfloat16)
    end_count = reset_count[-1]
    carry_weight = jnp.where((reset_count == 0)[:, None], jnp.exp(running), 0.0)
    tail_weight = jnp.where(
        (reset_count == end_count)[:, None], jnp.exp(running[-1][None, :] - running), 0.0
    )
    block_decay = jnp.where(end_count == 0, jnp.exp(running[-1]), 0.0)
    return (mixing, carry_weight, tail_weight, block_decay)


def chain_link(earlier, later):
    return (earlier[0] * later[0], later[0][:, None, None] * earlier[1] + later[1])


def local(
    ssm_input,
    gate_z,
    b_proj,
    c_proj,
    step_size,
    log_decay,
    skip_d,
    norm_gain,
    w_out,
    d_out,
    game_lengths,
):
    seq_len = ssm_input.shape[1]
    local_width = ssm_input.shape[2]
    heads_here = step_size.shape[2]
    head_dim = local_width // heads_here
    state_dim = b_proj.shape[2]
    block_len = min(512, seq_len)
    count_blocks = seq_len // block_len
    total_width = local_width * lax.axis_size("chan")
    x_heads = ssm_input[0].reshape(seq_len, heads_here, head_dim)
    c_rows = c_proj[0]
    b_rows = b_proj[0]
    dt_rows = step_size[0]
    lengths = game_lengths[0]
    starts = jnp.cumsum(lengths) - lengths
    sequence_positions = lax.axis_index(SEQ) * seq_len + jnp.arange(seq_len, dtype=jnp.int32)
    resets = jnp.any(sequence_positions[:, None] == starts[None, :], axis=1).astype(jnp.int32)

    def blocked(array):
        return array.reshape((count_blocks, block_len) + array.shape[1:])

    zero_state = jnp.zeros((heads_here, state_dim, head_dim), jnp.float32)
    unit_decay = jnp.ones((heads_here,), jnp.float32)

    def forward_step(state_pair, block_inputs):
        local_state, before = state_pair
        x_block, c_block, b_block, dt_block, decay_block, reset_block = block_inputs
        mixing, carry_weight, tail_weight, block_decay = block_parts(
            c_block, b_block, dt_block, decay_block, reset_block
        )
        inside = jnp.einsum("hts,shp->thp", mixing, x_block, preferred_element_type=jnp.float32)
        carried = carry_weight[:, :, None] * jnp.einsum(
            "tn,hnp->thp", c_block.astype(jnp.float32), local_state
        )
        scaled = ((tail_weight * dt_block)[:, :, None] * x_block).astype(jnp.bfloat16)
        fresh_state = jnp.einsum("sn,shp->hnp", b_block, scaled, preferred_element_type=jnp.float32)
        new_pair = (block_decay[:, None, None] * local_state + fresh_state, before * block_decay)
        return (
            new_pair,
            (
                inside + carried,
                carry_weight * before[None, :],
                mixing,
                carry_weight,
                tail_weight,
                block_decay,
            ),
        )

    forward_inputs = (
        blocked(x_heads),
        blocked(c_rows),
        blocked(b_rows),
        blocked(dt_rows),
        blocked(log_decay[0]),
        blocked(resets),
    )
    (dev_state, dev_decay), (
        ssd_blocks,
        incoming_weight,
        mixings,
        carry_weights,
        tail_weights,
        block_decays,
    ) = lax.scan(forward_step, (zero_state, unit_decay), forward_inputs)
    _, incoming = prefix_by_axis(
        (dev_decay, dev_state), SEQ, chain_link, (unit_decay, zero_state), False
    )
    from_left = jnp.einsum("tn,hnp->thp", c_rows.astype(jnp.float32), incoming)
    ssd_out = (
        ssd_blocks.reshape(seq_len, heads_here, head_dim)
        + incoming_weight.reshape(seq_len, heads_here)[:, :, None] * from_left
    )
    ssd_out = ssd_out + skip_d[None, :, None] * x_heads.astype(jnp.float32)
    gate_act = jax.nn.silu(gate_z[0].astype(jnp.float32))
    gated = ssd_out.reshape(seq_len, local_width) * gate_act
    square_total = lax.psum(jnp.sum(gated * gated, axis=1), "chan")
    inv_rms = lax.rsqrt(square_total / total_width + NORM_EPS)
    normed = (gated * norm_gain).astype(jnp.bfloat16)
    w_cols = w_out
    projected = sent_and_summed(
        lax.dot_general(
            w_cols, normed, (((0,), (1,)), ((), ())), preferred_element_type=jnp.float32
        ).astype(jnp.bfloat16),
        "chan",
        0,
    ).T
    out = (inv_rms[:, None] * projected).astype(jnp.bfloat16)[None]
    cotangent = d_out[0]
    w_cols = w_out
    pulled = lax.dot_general(
        lax.all_gather(cotangent, "chan", axis=1, tiled=True),
        w_cols,
        (((1,), (1,)), ((), ())),
        preferred_element_type=jnp.float32,
    )
    out_dot = lax.psum(jnp.sum(cotangent.astype(jnp.float32) * projected, axis=1), "chan")
    d_normed = inv_rms[:, None] * pulled
    gain_local = jnp.sum(gated * d_normed, axis=0)
    d_ssd = (
        (norm_gain * d_normed - (inv_rms**3 * out_dot / total_width)[:, None] * gated) * gate_act
    ).astype(jnp.bfloat16)
    d_heads = d_ssd.reshape(seq_len, heads_here, head_dim)
    skip_local = jnp.sum(d_heads.astype(jnp.float32) * x_heads.astype(jnp.float32), axis=(0, 2))
    grad_gain, grad_skip = (taken_together(gain_local, SEQ_DP), taken_together(skip_local, SEQ_DP))

    def backward_step(state_pair, block_inputs):
        local_adjoint, later_decay = state_pair
        d_block, c_block, b_block, dt_block, mixing, carry_weight, tail_weight, block_decay = (
            block_inputs
        )
        inside = jnp.einsum("hts,thp->shp", mixing, d_block, preferred_element_type=jnp.float32)
        carried = (dt_block * tail_weight)[:, :, None] * jnp.einsum(
            "sn,hnp->shp", b_block.astype(jnp.float32), local_adjoint
        )
        weighted = (carry_weight[:, :, None] * d_block).astype(jnp.bfloat16)
        fresh_adjoint = jnp.einsum(
            "tn,thp->hnp", c_block, weighted, preferred_element_type=jnp.float32
        )
        new_pair = (
            fresh_adjoint + block_decay[:, None, None] * local_adjoint,
            later_decay * block_decay,
        )
        return (new_pair, (inside + carried, dt_block * tail_weight * later_decay[None, :]))

    backward_inputs = (
        blocked(d_heads),
        blocked(c_rows),
        blocked(b_rows),
        blocked(dt_rows),
        mixings,
        carry_weights,
        tail_weights,
        block_decays,
    )
    (dev_adjoint, _), (grad_blocks, outgoing_weight) = lax.scan(
        backward_step, (zero_state, unit_decay), backward_inputs, reverse=True
    )
    _, from_right = prefix_by_axis(
        (dev_decay, dev_adjoint), SEQ, chain_link, (unit_decay, zero_state), True
    )
    right_terms = jnp.einsum("sn,hnp->shp", b_rows.astype(jnp.float32), from_right)
    grad_heads = (
        grad_blocks.reshape(seq_len, heads_here, head_dim)
        + outgoing_weight.reshape(seq_len, heads_here)[:, :, None] * right_terms
    )
    grad_heads = grad_heads + skip_d[None, :, None] * d_heads.astype(jnp.float32)
    grad_x = grad_heads.astype(jnp.bfloat16).reshape(1, seq_len, local_width)
    return (out, grad_x, grad_gain, grad_skip)


def solution(mesh):
    finer = Mesh(
        mesh.devices.reshape(4, 8, mesh.shape["chan"], mesh.shape["dp"]),
        ("seq_0", "seq_1", "chan", "dp"),
    )
    return jax.shard_map(
        local,
        mesh=finer,
        in_specs=(
            P("dp", SEQ, "chan"),
            P("dp", SEQ, "chan"),
            P("dp", SEQ, None),
            P("dp", SEQ, None),
            P("dp", SEQ, "chan"),
            P("dp", SEQ, "chan"),
            P("chan"),
            P("chan"),
            P("chan", None),
            P("dp", SEQ, "chan"),
            P("dp", None),
        ),
        out_specs=(P("dp", SEQ, "chan"), P("dp", SEQ, "chan"), P("chan"), P("chan")),
        check_vma=False,
    )
```

profile of v0, /device:TPU:8, one launch (start us, length us, event | category | flops | bytes accessed | tf_op | source)
XLA Modules:
  0.0 205.9 jit_solution(17596666255649511182)
XLA Ops:
  7.2 0.0 all-gather.9.cloned.1.call-start
  7.3 1.0 reduce-window_clone.1
  8.3 0.7 subtract_bitcast_fusion
  8.9 0.1 compare_reduce_fusion
  9.0 0.1 copy.85
  9.1 0.2 broadcast_in_dim.163
  9.3 0.5 slice.212
  9.8 0.1 reduce.5
  10.6 0.8 copy.86
  11.4 0.2 reduce_window_sum.27
  11.6 0.7 broadcast_compare_fusion.1
  12.2 0.8 copy.89
  13.0 0.1 exponential_select_fusion
  13.2 0.1 copy.94
  13.4 0.9 fusion.16
  14.3 0.1 copy.95
  14.4 0.8 fusion.14
  15.3 19.1 %all-gather.3 = bf16[8,1,8]{2,1,0:T(2,128)(2,1)S(1)} all-gather(bf16[1,1,8]{2,1,0:T(2,128)(2,1)S(1)} %get-tuple-element.116), channel_id=1, replica_groups=mesh['seq_0'=4,'seq_1'=8,'chan'=8,'dp'=2] {'seq_1'}, dimensions={0}, use_global_device_ids=true | all-gather | bytes 144 | tf_op jit(solution)/shard_map/all_gather | solution.py:24
  34.4 0.5 convert_bitcast_fusion.2
  34.9 7.0 %all-gather.4 = bf16[4,1,8]{2,1,0:T(2,128)(2,1)S(1)} all-gather(bf16[1,1,8]{2,1,0:T(2,128)(2,1)S(1)} %get-tuple-element.121), channel_id=1, replica_groups=mesh['seq_0'=4,'seq_1'=8,'chan'=8,'dp'=2] {'seq_0'}, dimensions={0}, use_global_device_ids=true | all-gather | bytes 80 | tf_op jit(solution)/shard_map/all_gather | solution.py:24
  41.9 0.1 copy.91
  42.0 0.1 copy.87
  42.1 0.1 copy.96
  42.3 0.5 broadcast_select_fusion.7
  42.8 0.5 fusion.179
  43.4 0.1 fusion.147
  43.5 0.1 fusion.154
  43.6 0.2 fusion.9
  43.8 16.6 %all-gather.9.cloned.1.call-done = bf16[64,128,64]{1,2,0:T(8,128)(2,1)} async-done(((bf16[8,128,64]{1,2,0:T(8,128)(2,1)}), bf16[64,128,64]{1,2,0:T(8,128)(2,1)}) %all-gather.9.cloned.1.call-update) | async-done | bytes 1048592 | tf_op jit(solution)/shard_map/all_gather | solution.py:24
  60.5 1.6 fusion.79
  62.1 13.1 %all_gather.41 = bf16[4,8,128,64]{2,3,1,0:T(8,128)(2,1)S(1)} all-gather(bf16[1,8,128,64]{2,3,1,0:T(8,128)(2,1)S(1)} %fusion.79), channel_id=1, replica_groups=mesh['seq_0'=4,'seq_1'=8,'chan'=8,'dp'=2] {'seq_0'}, dimensions={0}, use_global_device_ids=true | all-gather | bytes 655360 | tf_op jit(solution)/shard_map/all_gather | solution.py:24
  75.2 1.9 fusion.8
  77.2 0.9 multiply_reduce_fusion.1
  78.1 0.8 copy.97
  79.0 1.4 convolution_convert_fusion
  80.4 0.8 copy.110
  81.2 7.6 %all-to-all-start = ((bf16[8,256,128]{1,2,0:T(8,128)(2,1)}), bf16[8,256,128]{1,2,0:T(8,128)(2,1)S(1)}, u32[]{:S(2)}, u32[]{:S(2)}) async-start(bf16[8,256,128]{1,2,0:T(8,128)(2,1)} %bitcast.430), calls=%async_computation | async-start | bytes 1048576 | tf_op jit(solution)/shard_map/all_to_all | solution.py:47
  88.9 0.1 copy.100
  89.0 29.6 %all-gather.1 = bf16[1,128,2048]{2,1,0:T(8,128)(2,1)S(1)} all-gather(bf16[1,128,256]{2,1,0:T(8,128)(2,1)S(1)} %copy-done.6), channel_id=3, replica_groups=mesh['seq_0'=4,'seq_1'=8,'chan'=8,'dp'=2] {'chan'}, dimensions={2}, use_global_device_ids=true | all-gather | bytes 589824 | tf_op jit(solution)/shard_map/all_gather | solution.py:196
  118.6 0.1 convert_reduce_fusion
  118.7 0.9 fusion.88
  119.7 16.8 %all-reduce = (f32[128]{0:T(128)S(1)}, f32[128]{0:T(128)S(1)}) all-reduce(f32[128]{0:T(128)} %get-tuple-element.140, f32[128]{0:T(128)S(1)} %fusion.88), channel_id=1, replica_groups=mesh['seq_0'=4,'seq_1'=8,'chan'=8,'dp'=2] {'chan'}, use_global_device_ids=true, to_apply=%region_5.6 | all-reduce | flops 256 | bytes 2048 | tf_op jit(solution)/shard_map/psum | solution.py:181
  136.6 2.0 fusion.18
  138.7 0.1 copy.101
  138.8 0.8 fusion.13
  139.7 9.3 %all-gather.5 = bf16[4,1,8]{2,1,0:T(2,128)(2,1)S(1)} all-gather(bf16[1,1,8]{2,1,0:T(2,128)(2,1)S(1)} %copy-done.28), channel_id=1, replica_groups=mesh['seq_0'=4,'seq_1'=8,'chan'=8,'dp'=2] {'seq_0'}, dimensions={0}, use_global_device_ids=true | all-gather | bytes 80 | tf_op jit(solution)/shard_map/all_gather | solution.py:24
  149.0 0.2 fusion.7
  149.2 0.1 reduce_sum.76
  149.3 0.1 reduce_sum.77
  149.4 0.6 broadcast_in_dim.174
  150.0 6.1 %all-to-all-start.2 = ((f32[64,1,8]{2,1,0:T(1,128)}), f32[64,1,8]{2,1,0:T(1,128)S(1)}, u32[]{:S(2)}, u32[]{:S(2)}) async-start(f32[64,1,8]{2,1,0:T(1,128)} %broadcast_in_dim.174), calls=%async_computation.2 | async-start | bytes 65536 | tf_op jit(solution)/shard_map/all_to_all | solution.py:53
  156.1 8.5 %all-to-all-done.2 = f32[64,1,8]{2,1,0:T(1,128)S(1)} async-done(((f32[64,1,8]{2,1,0:T(1,128)}), f32[64,1,8]{2,1,0:T(1,128)S(1)}, u32[]{:S(2)}, u32[]{:S(2)}) %all-to-all-start.2) | async-done | bytes 2080 | tf_op jit(solution)/shard_map/all_to_all | solution.py:53
  164.6 0.7 broadcast_in_dim.173
  165.3 5.4 %all-to-all-start.1 = ((f32[64,1,512]{2,1,0:T(1,128)}), f32[64,1,512]{2,1,0:T(1,128)S(1)}, u32[]{:S(2)}, u32[]{:S(2)}) async-start(f32[64,1,512]{2,1,0:T(1,128)} %broadcast_in_dim.173), calls=%async_computation.1 | async-start | bytes 262144 | tf_op jit(solution)/shard_map/all_to_all | solution.py:53
  170.8 0.1 copy.99
  170.9 0.7 fusion.145
  171.6 0.6 reduce_sum.78
  172.2 8.5 %all-to-all-done.1 = f32[64,1,512]{2,1,0:T(1,128)S(1)} async-done(((f32[64,1,512]{2,1,0:T(1,128)}), f32[64,1,512]{2,1,0:T(1,128)S(1)}, u32[]{:S(2)}, u32[]{:S(2)}) %all-to-all-start.1) | async-done | bytes 131104 | tf_op jit(solution)/shard_map/all_to_all | solution.py:53
  180.7 0.7 reduce_sum.74
  181.5 1.6 fusion.62
  183.1 12.8 %all_gather.46 = bf16[4,8,128,64]{2,3,1,0:T(8,128)(2,1)S(1)} all-gather(bf16[1,8,128,64]{2,3,1,0:T(8,128)(2,1)S(1)} %fusion.62), channel_id=1, replica_groups=mesh['seq_0'=4,'seq_1'=8,'chan'=8,'dp'=2] {'seq_0'}, dimensions={0}, use_global_device_ids=true | all-gather | bytes 655360 | tf_op jit(solution)/shard_map/all_gather | solution.py:24
  195.9 1.9 fusion.6
  197.9 0.4 fusion.12
  198.3 0.8 copy.104
  (86 shorter events, 0.5 us)
Async XLA Ops:
  7.2 71.8 %copy-start = (bf16[512,2048]{1,0:T(8,128)(2,1)S(1)}, bf16[512,2048]{1,0:T(8,128)(2,1)}, u32[]{:S(2)}) copy-start(bf16[512,2048]{1,0:T(8,128)(2,1)} %param.19) | copy-start | bytes 6291460
  7.2 34.7 %copy-start.1 = (bf16[1,128,512]{2,1,0:T(8,128)(2,1)S(1)}, bf16[1,128,512]{2,1,0:T(8,128)(2,1)}, u32[]{:S(2)}) copy-start(bf16[1,128,512]{2,1,0:T(8,128)(2,1)} %param.11) | copy-start | bytes 393220
  7.2 7.2 %copy-start.4 = (bf16[1,128,128]{2,1,0:T(8,128)(2,1)S(1)}, bf16[1,128,128]{2,1,0:T(8,128)(2,1)}, u32[]{:S(2)}) copy-start(bf16[1,128,128]{2,1,0:T(8,128)(2,1)} %param.13) | copy-start | bytes 98308
  7.2 34.9 %copy-start.7 = (bf16[1,128,512]{2,1,0:T(8,128)(2,1)S(1)}, bf16[1,128,512]{2,1,0:T(8,128)(2,1)}, u32[]{:S(2)}) copy-start(bf16[1,128,512]{2,1,0:T(8,128)(2,1)} %param.12) | copy-start | bytes 393220
  7.2 36.3 %copy-start.2 = (bf16[1,128,128]{2,1,0:T(8,128)(2,1)S(1)}, bf16[1,128,128]{2,1,0:T(8,128)(2,1)}, u32[]{:S(2)}) copy-start(bf16[1,128,128]{2,1,0:T(8,128)(2,1)} %param.14) | copy-start | bytes 98308
  7.2 53.2 %all-gather.9.cloned.1.call-start = ((), (), s32[]{:S(2)}) async-start(), calls=%async_computation.3 | async-start | bytes 1179648 | tf_op jit(solution)/shard_map/all_gather | solution.py:24
  11.6 30.3 %copy-start.24 = (f32[8]{0:T(128)}, f32[8]{0:T(128)S(1)}, u32[]{:S(2)}) copy-start(f32[8]{0:T(128)S(1)} %fusion.160) | copy-start | bytes 100
  42.1 35.1 %copy-start.22 = (f32[8,128]{1,0:T(8,128)}, f32[8,128]{1,0:T(8,128)S(1)}, u32[]{:S(2)}) copy-start(f32[8,128]{1,0:T(8,128)S(1)} %copy.87) | copy-start | bytes 12292
  43.4 33.8 %copy-start.12 = (f32[8]{0:T(128)}, f32[8]{0:T(128)S(1)}, u32[]{:S(2)}) copy-start(f32[8]{0:T(128)S(1)} %get-tuple-element.125) | copy-start | bytes 100
  43.4 33.8 %copy-start.14 = (f32[8]{0:T(128)}, f32[8]{0:T(128)S(1)}, u32[]{:S(2)}) copy-start(f32[8]{0:T(128)S(1)} %get-tuple-element.126) | copy-start | bytes 100
  43.4 33.8 %copy-start.16 = (f32[8]{0:T(128)}, f32[8]{0:T(128)S(1)}, u32[]{:S(2)}) copy-start(f32[8]{0:T(128)S(1)} %get-tuple-element.127) | copy-start | bytes 100
  43.4 33.8 %copy-start.18 = (f32[8]{0:T(128)}, f32[8]{0:T(128)S(1)}, u32[]{:S(2)}) copy-start(f32[8]{0:T(128)S(1)} %get-tuple-element.128) | copy-start | bytes 100
  43.5 33.7 %copy-start.10 = (pred[128,128]{1,0:T(8,128)(4,1)}, pred[128,128]{1,0:T(8,128)(4,1)S(1)}, u32[]{:S(2)}) copy-start(pred[128,128]{1,0:T(8,128)(4,1)S(1)} %fusion.147) | copy-start | bytes 49156
  43.6 33.6 %copy-start.8 = (f32[128,128]{1,0:T(8,128)}, f32[128,128]{1,0:T(8,128)S(1)}, u32[]{:S(2)}) copy-start(f32[128,128]{1,0:T(8,128)S(1)} %fusion.154) | copy-start | bytes 196612
  75.2 2.0 copy-start.20
  75.2 2.0 copy-start.31
  77.2 1.8 copy-start.30
  80.4 8.6 %copy-start.6 = (bf16[1,128,256]{2,1,0:T(8,128)(2,1)S(1)}, bf16[1,128,256]{2,1,0:T(8,128)(2,1)}, u32[]{:S(2)}) copy-start(bf16[1,128,256]{2,1,0:T(8,128)(2,1)} %param.20) | copy-start | bytes 196612
  81.2 37.4 %all-to-all-start = ((bf16[8,256,128]{1,2,0:T(8,128)(2,1)}), bf16[8,256,128]{1,2,0:T(8,128)(2,1)S(1)}, u32[]{:S(2)}, u32[]{:S(2)}) async-start(bf16[8,256,128]{1,2,0:T(8,128)(2,1)} %bitcast.430), calls=%async_computation | async-start | bytes 1048576 | tf_op jit(solution)/shard_map/all_to_all | solution.py:47
  88.8 92.6 %all-gather.11.cloned.1.call-start = ((), (), s32[]{:S(2)}) async-start(), calls=%async_computation.4 | async-start | bytes 1179648 | tf_op jit(solution)/shard_map/all_gather | solution.py:24
  136.5 2.3 %copy-start.3 = (bf16[1,128,128]{2,1,0:T(8,128)(2,1)S(1)}, bf16[1,128,128]{2,1,0:T(8,128)(2,1)}, u32[]{:S(2)}) copy-start(bf16[1,128,128]{2,1,0:T(8,128)(2,1)} %param.14) | copy-start | bytes 98308
  136.5 2.3 %copy-start.25 = (f32[8]{0:T(128)S(1)}, f32[8]{0:T(128)}, u32[]{:S(2)}) copy-start(f32[8]{0:T(128)} %copy-done.24) | copy-start | bytes 100
  136.5 3.1 %copy-start.28 = (bf16[1,1,8]{2,1,0:T(2,128)(2,1)S(1)}, bf16[1,1,8]{2,1,0:T(2,128)(2,1)}, u32[]{:S(2)}) copy-start(bf16[1,1,8]{2,1,0:T(2,128)(2,1)} %get-tuple-element.120) | copy-start | bytes 52
  136.5 12.5 %copy-start.5 = (bf16[1,128,128]{2,1,0:T(8,128)(2,1)S(1)}, bf16[1,128,128]{2,1,0:T(8,128)(2,1)}, u32[]{:S(2)}) copy-start(bf16[1,128,128]{2,1,0:T(8,128)(2,1)} %param.13) | copy-start | bytes 98308
  138.5 42.9 %copy-start.13 = (f32[8]{0:T(128)S(1)}, f32[8]{0:T(128)}, u32[]{:S(2)}) copy-start(f32[8]{0:T(128)} %copy-done.12) | copy-start | bytes 100
  138.6 42.9 %copy-start.15 = (f32[8]{0:T(128)S(1)}, f32[8]{0:T(128)}, u32[]{:S(2)}) copy-start(f32[8]{0:T(128)} %copy-done.14) | copy-start | bytes 100
  138.6 42.9 %copy-start.17 = (f32[8]{0:T(128)S(1)}, f32[8]{0:T(128)}, u32[]{:S(2)}) copy-start(f32[8]{0:T(128)} %copy-done.16) | copy-start | bytes 100
  138.6 42.9 %copy-start.19 = (f32[8]{0:T(128)S(1)}, f32[8]{0:T(128)}, u32[]{:S(2)}) copy-start(f32[8]{0:T(128)} %copy-done.18) | copy-start | bytes 100
  138.6 42.9 %copy-start.26 = (f32[8]{0:T(128)S(1)}, f32[8]{0:T(128)}, u32[]{:S(2)}) copy-start(f32[8]{0:T(128)} %get-tuple-element.119) | copy-start | bytes 100
  138.6 42.9 %copy-start.27 = (f32[8]{0:T(128)S(1)}, f32[8]{0:T(128)}, u32[]{:S(2)}) copy-start(f32[8]{0:T(128)} %get-tuple-element.122) | copy-start | bytes 100
  138.6 57.3 %copy-start.29 = (f32[8]{0:T(128)S(1)}, f32[8]{0:T(128)}, u32[]{:S(2)}) copy-start(f32[8]{0:T(128)} %get-tuple-element.117) | copy-start | bytes 100
  150.0 14.6 %all-to-all-start.2 = ((f32[64,1,8]{2,1,0:T(1,128)}), f32[64,1,8]{2,1,0:T(1,128)S(1)}, u32[]{:S(2)}, u32[]{:S(2)}) async-start(f32[64,1,8]{2,1,0:T(1,128)} %broadcast_in_dim.174), calls=%async_computation.2 | async-start | bytes 65536 | tf_op jit(solution)/shard_map/all_to_all | solution.py:53
  165.3 15.4 %all-to-all-start.1 = ((f32[64,1,512]{2,1,0:T(1,128)}), f32[64,1,512]{2,1,0:T(1,128)S(1)}, u32[]{:S(2)}, u32[]{:S(2)}) async-start(f32[64,1,512]{2,1,0:T(1,128)} %broadcast_in_dim.173), calls=%async_computation.1 | async-start | bytes 262144 | tf_op jit(solution)/shard_map/all_to_all | solution.py:53
  195.9 2.0 copy-start.9
  195.9 2.0 copy-start.11
  195.9 2.0 copy-start.21
  195.9 2.0 copy-start.23
  195.9 2.0 copy-start.32
Sparse Core Ops, SparseCore 0:
  15.4 45.0 all-gather.8
  139.8 38.7 all-gather.10
where the time goes:
time: 207 us; the launch traced here: 206 us
  blocking collectives  108 us (52%)
  waiting for transfers between devices  33.7 us (16%)
  starting transfers between devices  19.1 us (9%)
  between operations  15.3 us (7%)
  other arithmetic  12 us (6%)
  matrix products  10.7 us (5%)
  local copies, waits for them, and re-layouts  7.31 us (4%)
    all_gather x5, blocking collectives, prefix_by_axis(): lax.all_gather(part.astype(kind), axis)  61.2 us
    all_gather x1, blocking collectives, local(): lax.all_gather(cotangent, 'chan', axis=1, tiled=True)  29.6 us
    all_to_all x2, waiting for transfers between devices, copy_for_each(): lax.all_to_all(jnp.broadcast_to(value[None], (length, *value.shape)), axi...  17.1 us
    psum x1, blocking collectives, local(): square_total = lax.psum(jnp.sum(gated * gated, axis=1), 'chan')  16.8 us
    all_gather x2, waiting for transfers between devices, prefix_by_axis(): lax.all_gather(part.astype(kind), axis)  16.6 us
    all_to_all x2, starting transfers between devices, copy_for_each(): lax.all_to_all(jnp.broadcast_to(value[None], (length, *value.shape)), axi...  11.4 us
    all_to_all x1, starting transfers between devices, sent_and_summed(): lax.all_to_all(in_blocks(value, dim, length), axis, 0, 0, tiled=True)  7.55 us
  transfers between devices with their start and end apart: 5, of which 3 were waited for; matrix products, arithmetic and copies ran while one was open for 3% of the time, Pallas kernels for 0%

commit v1 on v0

--- a/solution.py
+++ b/solution.py
@@ -178,7 +178,11 @@
     ssd_out = ssd_out + skip_d[None, :, None] * x_heads.astype(jnp.float32)
     gate_act = jax.nn.silu(gate_z[0].astype(jnp.float32))
     gated = ssd_out.reshape(seq_len, local_width) * gate_act
-    square_total = lax.psum(jnp.sum(gated * gated, axis=1), "chan")
+
+    def _lay_figure(buf):
+        return lax.all_gather(buf, axis_name="chan").sum(axis=0)
+
+    square_total = _lay_figure(jnp.sum(gated * gated, axis=1))
     inv_rms = lax.rsqrt(square_total / total_width + NORM_EPS)
     normed = (gated * norm_gain).astype(jnp.bfloat16)
     w_cols = w_out

time: 207 us -> 221 us (1.068)
  the two profiles are of different devices: /device:TPU:8 before, /device:TPU:16 now
where the time goes in v1:
time: 221 us; the launch traced here: 220 us
  blocking collectives  120 us (54%)
  waiting for transfers between devices  33.8 us (15%)
  starting transfers between devices  20.8 us (9%)
  between operations  15.3 us (7%)
  other arithmetic  13.9 us (6%)
  matrix products  9.75 us (4%)
  local copies, waits for them, and re-layouts  6.56 us (3%)
    all_gather x5, blocking collectives, prefix_by_axis(): lax.all_gather(part.astype(kind), axis)  60 us
    all_gather x1, blocking collectives, local(): lax.all_gather(cotangent, 'chan', axis=1, tiled=True)  29.8 us
    all_gather x2, waiting for transfers between devices, prefix_by_axis(): lax.all_gather(part.astype(kind), axis)  17.4 us
    all_to_all x2, waiting for transfers between devices, copy_for_each(): lax.all_to_all(jnp.broadcast_to(value[None], (length, *value.shape)), axi...  16.4 us
    all_gather x1, blocking collectives, _lay_figure(): return lax.all_gather(buf, axis_name='chan').sum(axis=0)  15.8 us
    psum x1, blocking collectives, local(): lax.psum(jnp.sum(cotangent.astype(jnp.float32) * projected, axis=1), 'chan')  14.6 us
    all_to_all x2, starting transfers between devices, copy_for_each(): lax.all_to_all(jnp.broadcast_to(value[None], (length, *value.shape)), axi...  13.4 us
    all_to_all x1, starting transfers between devices, sent_and_summed(): lax.all_to_all(in_blocks(value, dim, length), axis, 0, 0, tiled=True)  7.38 us
  transfers between devices with their start and end apart: 5, of which 3 were waited for; matrix products, arithmetic and copies ran while one was open for 3% of the time, Pallas kernels for 0%

profile of v1, /device:TPU:16, one launch (start us, length us, event | category | flops | bytes accessed | tf_op | source)
XLA Modules:
  0.0 220.3 jit_solution(4687219020408340689)
XLA Ops:
  7.3 1.0 reduce-window_clone.1
  8.3 0.7 subtract_bitcast_fusion
  8.9 0.1 compare_reduce_fusion
  9.0 0.1 copy.85
  9.1 0.2 broadcast_in_dim.163
  9.3 0.5 slice.212
  9.8 0.1 reduce.6
  10.6 0.8 copy.86
  11.4 0.2 reduce_window_sum.27
  11.6 0.7 broadcast_compare_fusion.1
  12.2 0.8 copy.89
  13.0 0.1 exponential_select_fusion
  13.2 0.1 copy.94
  13.4 0.9 fusion.16
  14.3 0.1 copy.95
  14.4 0.8 fusion.14
  15.3 16.3 %all-gather.4 = bf16[8,1,8]{2,1,0:T(2,128)(2,1)S(1)} all-gather(bf16[1,1,8]{2,1,0:T(2,128)(2,1)S(1)} %get-tuple-element.116), channel_id=1, replica_groups=mesh['seq_0'=4,'seq_1'=8,'chan'=8,'dp'=2] {'seq_1'}, dimensions={0}, use_global_device_ids=true | all-gather | bytes 144 | tf_op jit(solution)/shard_map/all_gather | solution.py:24
  31.6 0.5 convert_bitcast_fusion.2
  32.1 7.8 %all-gather.5 = bf16[4,1,8]{2,1,0:T(2,128)(2,1)S(1)} all-gather(bf16[1,1,8]{2,1,0:T(2,128)(2,1)S(1)} %get-tuple-element.121), channel_id=1, replica_groups=mesh['seq_0'=4,'seq_1'=8,'chan'=8,'dp'=2] {'seq_0'}, dimensions={0}, use_global_device_ids=true | all-gather | bytes 80 | tf_op jit(solution)/shard_map/all_gather | solution.py:24
  40.0 0.1 copy.91
  40.2 0.1 copy.96
  40.4 0.6 broadcast_select_fusion.7
  41.0 0.6 fusion.179
  41.6 0.1 fusion.147
  41.7 0.1 fusion.154
  41.8 0.2 fusion.9
  42.0 17.4 %all-gather.11.cloned.1.call-done = bf16[64,128,64]{1,2,0:T(8,128)(2,1)} async-done(((bf16[8,128,64]{1,2,0:T(8,128)(2,1)}), bf16[64,128,64]{1,2,0:T(8,128)(2,1)}) %all-gather.11.cloned.1.call-update) | async-done | bytes 1048592 | tf_op jit(solution)/shard_map/all_gather | solution.py:24
  59.4 1.6 fusion.79
  61.1 13.1 %all_gather.47 = bf16[4,8,128,64]{2,3,1,0:T(8,128)(2,1)S(1)} all-gather(bf16[1,8,128,64]{2,3,1,0:T(8,128)(2,1)S(1)} %fusion.79), channel_id=1, replica_groups=mesh['seq_0'=4,'seq_1'=8,'chan'=8,'dp'=2] {'seq_0'}, dimensions={0}, use_global_device_ids=true | all-gather | bytes 655360 | tf_op jit(solution)/shard_map/all_gather | solution.py:24
  74.2 1.9 fusion.8
  76.2 0.9 multiply_reduce_fusion.1
  77.1 0.1 copy.97
  77.3 0.5 convolution_convert_fusion
  77.8 0.8 copy.110
  78.6 7.4 %all-to-all-start = ((bf16[8,256,128]{1,2,0:T(8,128)(2,1)}), bf16[8,256,128]{1,2,0:T(8,128)(2,1)S(1)}, u32[]{:S(2)}, u32[]{:S(2)}) async-start(bf16[8,256,128]{1,2,0:T(8,128)(2,1)} %bitcast.431), calls=%async_computation | async-start | bytes 1048576 | tf_op jit(solution)/shard_map/all_to_all | solution.py:47
  86.1 0.1 copy.100
  86.2 29.8 %all-gather.2 = bf16[1,128,2048]{2,1,0:T(8,128)(2,1)S(1)} all-gather(bf16[1,128,256]{2,1,0:T(8,128)(2,1)} %param.20), channel_id=4, replica_groups=mesh['seq_0'=4,'seq_1'=8,'chan'=8,'dp'=2] {'chan'}, dimensions={2}, use_global_device_ids=true | all-gather | bytes 589824 | tf_op jit(solution)/shard_map/all_gather | solution.py:200
  116.0 15.8 %all-gather.6 = f32[8,1,128]{2,1,0:T(1,128)S(1)} all-gather(f32[1,1,128]{2,1,0:T(1,128)} %bitcast.446), channel_id=3, replica_groups=mesh['seq_0'=4,'seq_1'=8,'chan'=8,'dp'=2] {'chan'}, dimensions={0}, use_global_device_ids=true | all-gather | bytes 4608 | tf_op jit(solution)/shard_map/all_gather | solution.py:183
  131.8 0.5 reduce_sum.80
  132.3 0.7 add_rsqrt_fusion
  133.1 1.6 fusion.88
  134.7 14.6 %psum.7 = f32[128]{0:T(128)S(1)} all-reduce(f32[128]{0:T(128)S(1)} %get-tuple-element.98), channel_id=1, replica_groups=mesh['seq_0'=4,'seq_1'=8,'chan'=8,'dp'=2] {'chan'}, use_global_device_ids=true, to_apply=%region_8.9 | all-reduce | flops 128 | bytes 1024 | tf_op jit(solution)/shard_map/psum | solution.py:205
  149.2 0.7 fusion.178
  149.9 1.9 fusion.18
  152.0 0.1 copy.101
  152.1 0.8 fusion.13
  153.0 9.4 %all-gather.7 = bf16[4,1,8]{2,1,0:T(2,128)(2,1)S(1)} all-gather(bf16[1,1,8]{2,1,0:T(2,128)(2,1)S(1)} %copy-done.28), channel_id=1, replica_groups=mesh['seq_0'=4,'seq_1'=8,'chan'=8,'dp'=2] {'seq_0'}, dimensions={0}, use_global_device_ids=true | all-gather | bytes 80 | tf_op jit(solution)/shard_map/all_gather | solution.py:24
  162.3 0.1 reduce_sum.86
  162.4 0.1 reduce_sum.87
  162.5 0.6 broadcast_in_dim.174
  163.1 7.1 %all-to-all-start.2 = ((f32[64,1,8]{2,1,0:T(1,128)}), f32[64,1,8]{2,1,0:T(1,128)S(1)}, u32[]{:S(2)}, u32[]{:S(2)}) async-start(f32[64,1,8]{2,1,0:T(1,128)} %broadcast_in_dim.174), calls=%async_computation.2 | async-start | bytes 65536 | tf_op jit(solution)/shard_map/all_to_all | solution.py:53
  170.2 7.8 %all-to-all-done.2 = f32[64,1,8]{2,1,0:T(1,128)S(1)} async-done(((f32[64,1,8]{2,1,0:T(1,128)}), f32[64,1,8]{2,1,0:T(1,128)S(1)}, u32[]{:S(2)}, u32[]{:S(2)}) %all-to-all-start.2) | async-done | bytes 2080 | tf_op jit(solution)/shard_map/all_to_all | solution.py:53
  178.1 0.7 broadcast_in_dim.173
  178.8 6.3 %all-to-all-start.1 = ((f32[64,1,512]{2,1,0:T(1,128)}), f32[64,1,512]{2,1,0:T(1,128)S(1)}, u32[]{:S(2)}, u32[]{:S(2)}) async-start(f32[64,1,512]{2,1,0:T(1,128)} %broadcast_in_dim.173), calls=%async_computation.1 | async-start | bytes 262144 | tf_op jit(solution)/shard_map/all_to_all | solution.py:53
  185.1 0.2 fusion.7
  185.3 0.1 copy.99
  185.4 0.6 reduce_sum.88
  186.0 8.5 %all-to-all-done.1 = f32[64,1,512]{2,1,0:T(1,128)S(1)} async-done(((f32[64,1,512]{2,1,0:T(1,128)}), f32[64,1,512]{2,1,0:T(1,128)S(1)}, u32[]{:S(2)}, u32[]{:S(2)}) %all-to-all-start.1) | async-done | bytes 131104 | tf_op jit(solution)/shard_map/all_to_all | solution.py:53
  194.6 0.7 reduce_sum.84
  195.3 1.6 fusion.62
  197.0 13.4 %all_gather.54 = bf16[4,8,128,64]{2,3,1,0:T(8,128)(2,1)S(1)} all-gather(bf16[1,8,128,64]{2,3,1,0:T(8,128)(2,1)S(1)} %fusion.62), channel_id=1, replica_groups=mesh['seq_0'=4,'seq_1'=8,'chan'=8,'dp'=2] {'seq_0'}, dimensions={0}, use_global_device_ids=true | all-gather | bytes 655360 | tf_op jit(solution)/shard_map/all_gather | solution.py:24
  210.4 1.9 fusion.6
  212.4 0.4 fusion.12
  212.7 0.8 copy.104
  (88 shorter events, 0.6 us)
Async XLA Ops:
  7.2 70.1 %copy-start = (bf16[512,2048]{1,0:T(8,128)(2,1)S(1)}, bf16[512,2048]{1,0:T(8,128)(2,1)}, u32[]{:S(2)}) copy-start(bf16[512,2048]{1,0:T(8,128)(2,1)} %param.19) | copy-start | bytes 6291460
  7.2 32.8 %copy-start.1 = (bf16[1,128,512]{2,1,0:T(8,128)(2,1)S(1)}, bf16[1,128,512]{2,1,0:T(8,128)(2,1)}, u32[]{:S(2)}) copy-start(bf16[1,128,512]{2,1,0:T(8,128)(2,1)} %param.11) | copy-start | bytes 393220
  7.2 7.2 %copy-start.4 = (bf16[1,128,128]{2,1,0:T(8,128)(2,1)S(1)}, bf16[1,128,128]{2,1,0:T(8,128)(2,1)}, u32[]{:S(2)}) copy-start(bf16[1,128,128]{2,1,0:T(8,128)(2,1)} %param.13) | copy-start | bytes 98308
  7.2 33.0 %copy-start.7 = (bf16[1,128,512]{2,1,0:T(8,128)(2,1)S(1)}, bf16[1,128,512]{2,1,0:T(8,128)(2,1)}, u32[]{:S(2)}) copy-start(bf16[1,128,512]{2,1,0:T(8,128)(2,1)} %param.12) | copy-start | bytes 393220
  7.2 34.4 %copy-start.2 = (bf16[1,128,128]{2,1,0:T(8,128)(2,1)S(1)}, bf16[1,128,128]{2,1,0:T(8,128)(2,1)}, u32[]{:S(2)}) copy-start(bf16[1,128,128]{2,1,0:T(8,128)(2,1)} %param.14) | copy-start | bytes 98308
  7.2 52.2 %all-gather.11.cloned.1.call-start = ((), (), s32[]{:S(2)}) async-start(), calls=%async_computation.3 | async-start | bytes 1179648 | tf_op jit(solution)/shard_map/all_gather | solution.py:24
  11.6 3.7 %copy-start.24 = (f32[8]{0:T(128)}, f32[8]{0:T(128)S(1)}, u32[]{:S(2)}) copy-start(f32[8]{0:T(128)S(1)} %fusion.160) | copy-start | bytes 100
  40.2 36.0 %copy-start.22 = (f32[8,128]{1,0:T(8,128)}, f32[8,128]{1,0:T(8,128)S(1)}, u32[]{:S(2)}) copy-start(f32[8,128]{1,0:T(8,128)S(1)} %copy.87) | copy-start | bytes 12292
  41.5 34.6 %copy-start.12 = (f32[8]{0:T(128)}, f32[8]{0:T(128)S(1)}, u32[]{:S(2)}) copy-start(f32[8]{0:T(128)S(1)} %get-tuple-element.125) | copy-start | bytes 100
  41.5 34.6 %copy-start.14 = (f32[8]{0:T(128)}, f32[8]{0:T(128)S(1)}, u32[]{:S(2)}) copy-start(f32[8]{0:T(128)S(1)} %get-tuple-element.126) | copy-start | bytes 100
  41.5 34.6 %copy-start.16 = (f32[8]{0:T(128)}, f32[8]{0:T(128)S(1)}, u32[]{:S(2)}) copy-start(f32[8]{0:T(128)S(1)} %get-tuple-element.127) | copy-start | bytes 100
  41.5 34.6 %copy-start.18 = (f32[8]{0:T(128)}, f32[8]{0:T(128)S(1)}, u32[]{:S(2)}) copy-start(f32[8]{0:T(128)S(1)} %get-tuple-element.128) | copy-start | bytes 100
  41.7 34.5 %copy-start.10 = (pred[128,128]{1,0:T(8,128)(4,1)}, pred[128,128]{1,0:T(8,128)(4,1)S(1)}, u32[]{:S(2)}) copy-start(pred[128,128]{1,0:T(8,128)(4,1)S(1)} %fusion.147) | copy-start | bytes 49156
  41.8 34.4 %copy-start.8 = (f32[128,128]{1,0:T(8,128)}, f32[128,128]{1,0:T(8,128)S(1)}, u32[]{:S(2)}) copy-start(f32[128,128]{1,0:T(8,128)S(1)} %fusion.154) | copy-start | bytes 196612
  74.2 2.0 copy-start.20
  74.2 2.0 copy-start.31
  76.2 1.1 copy-start.30
  77.3 1.3 copy-start.6
  78.6 54.4 %all-to-all-start = ((bf16[8,256,128]{1,2,0:T(8,128)(2,1)}), bf16[8,256,128]{1,2,0:T(8,128)(2,1)S(1)}, u32[]{:S(2)}, u32[]{:S(2)}) async-start(bf16[8,256,128]{1,2,0:T(8,128)(2,1)} %bitcast.431), calls=%async_computation | async-start | bytes 1048576 | tf_op jit(solution)/shard_map/all_to_all | solution.py:47
  86.0 109.3 %all-gather.13.cloned.1.call-start = ((), (), s32[]{:S(2)}) async-start(), calls=%async_computation.4 | async-start | bytes 1179648 | tf_op jit(solution)/shard_map/all_gather | solution.py:24
  149.9 2.2 %copy-start.3 = (bf16[1,128,128]{2,1,0:T(8,128)(2,1)S(1)}, bf16[1,128,128]{2,1,0:T(8,128)(2,1)}, u32[]{:S(2)}) copy-start(bf16[1,128,128]{2,1,0:T(8,128)(2,1)} %param.14) | copy-start | bytes 98308
  149.9 2.2 %copy-start.25 = (f32[8]{0:T(128)S(1)}, f32[8]{0:T(128)}, u32[]{:S(2)}) copy-start(f32[8]{0:T(128)} %copy-done.24) | copy-start | bytes 100
  149.9 3.1 %copy-start.28 = (bf16[1,1,8]{2,1,0:T(2,128)(2,1)S(1)}, bf16[1,1,8]{2,1,0:T(2,128)(2,1)}, u32[]{:S(2)}) copy-start(bf16[1,1,8]{2,1,0:T(2,128)(2,1)} %get-tuple-element.120) | copy-start | bytes 52
  149.9 35.2 %copy-start.5 = (bf16[1,128,128]{2,1,0:T(8,128)(2,1)S(1)}, bf16[1,128,128]{2,1,0:T(8,128)(2,1)}, u32[]{:S(2)}) copy-start(bf16[1,128,128]{2,1,0:T(8,128)(2,1)} %param.13) | copy-start | bytes 98308
  151.9 43.4 %copy-start.13 = (f32[8]{0:T(128)S(1)}, f32[8]{0:T(128)}, u32[]{:S(2)}) copy-start(f32[8]{0:T(128)} %copy-done.12) | copy-start | bytes 100
  151.9 43.4 %copy-start.15 = (f32[8]{0:T(128)S(1)}, f32[8]{0:T(128)}, u32[]{:S(2)}) copy-start(f32[8]{0:T(128)} %copy-done.14) | copy-start | bytes 100
  151.9 43.4 %copy-start.17 = (f32[8]{0:T(128)S(1)}, f32[8]{0:T(128)}, u32[]{:S(2)}) copy-start(f32[8]{0:T(128)} %copy-done.16) | copy-start | bytes 100
  151.9 43.4 %copy-start.19 = (f32[8]{0:T(128)S(1)}, f32[8]{0:T(128)}, u32[]{:S(2)}) copy-start(f32[8]{0:T(128)} %copy-done.18) | copy-start | bytes 100
  151.9 43.4 %copy-start.26 = (f32[8]{0:T(128)S(1)}, f32[8]{0:T(128)}, u32[]{:S(2)}) copy-start(f32[8]{0:T(128)} %get-tuple-element.119) | copy-start | bytes 100
  151.9 43.4 %copy-start.27 = (f32[8]{0:T(128)S(1)}, f32[8]{0:T(128)}, u32[]{:S(2)}) copy-start(f32[8]{0:T(128)} %get-tuple-element.122) | copy-start | bytes 100
  151.9 58.4 %copy-start.29 = (f32[8]{0:T(128)S(1)}, f32[8]{0:T(128)}, u32[]{:S(2)}) copy-start(f32[8]{0:T(128)} %get-tuple-element.117) | copy-start | bytes 100
  163.1 14.9 %all-to-all-start.2 = ((f32[64,1,8]{2,1,0:T(1,128)}), f32[64,1,8]{2,1,0:T(1,128)S(1)}, u32[]{:S(2)}, u32[]{:S(2)}) async-start(f32[64,1,8]{2,1,0:T(1,128)} %broadcast_in_dim.174), calls=%async_computation.2 | async-start | bytes 65536 | tf_op jit(solution)/shard_map/all_to_all | solution.py:53
  178.8 15.8 %all-to-all-start.1 = ((f32[64,1,512]{2,1,0:T(1,128)}), f32[64,1,512]{2,1,0:T(1,128)S(1)}, u32[]{:S(2)}, u32[]{:S(2)}) async-start(f32[64,1,512]{2,1,0:T(1,128)} %broadcast_in_dim.173), calls=%async_computation.1 | async-start | bytes 262144 | tf_op jit(solution)/shard_map/all_to_all | solution.py:53
  210.3 2.0 copy-start.9
  210.3 2.0 copy-start.11
  210.3 2.0 copy-start.21
  210.3 2.0 copy-start.23
  210.3 2.0 copy-start.32
Sparse Core Ops, SparseCore 0:
  15.4 43.9 all-gather.10
  153.1 38.1 all-gather.12
